TPU v7x, 32 devices: a whole 2x2x4 slice. The times are simulated.
32 devices in a mesh: row: 4 (over z), col: 8 (over y, x, core).
Axes of the slice: x: 2, y: 2, z: 4, core: 2. Of those that a mesh axis runs over, the one named last changes fastest.
Arguments:
- a_matrix: float32 [8192, 8192], P('row', 'col'), may hold values from -14 to 30, as said below
- b_matrix: float32 [4096, 4096], P('row', 'col'), may hold values from -14 to 30, as said below
- c_matrix: float32 [8192, 4096], P('row', 'col'), may hold values from -6 to 6
Outputs:
- a_swept: float32 [8192, 8192], P('row', 'col')
- c_swept: float32 [8192, 4096], P('row', 'col')
- b_next: float32 [4096, 4096], P('row', 'col')
Inputs may be any that keep to these rules, and one draw needn't show every extreme that they name: `a_matrix`: symmetric positive definite; its smallest eigenvalue is at least 1. `b_matrix`: symmetric positive definite; its smallest eigenvalue is at least 1.
All inputs are finite; a program needn't handle non-finite values. Where the computation divides by a largest or mean magnitude, that divisor is 1e-20 or more.
Results may differ from a plain program's by a relative error of at most 0.00012.
Values sent between devices are 32-bit elements; how exact they have to be, the bound alone decides.
A program may use at most 128 MiB of HBM per device.

v0:
```python
import functools

import jax
import jax.numpy as jnp
from jax import lax
from jax.experimental import pallas as pl
from jax.experimental.pallas import tpu as pltpu
from jax.sharding import PartitionSpec as P

PANEL = 256
PIVOT_ITERS = 6
STEPS_A = 2
STEPS_B = 16

EXACT = lax.Precision.HIGHEST
SPLIT = lax.Precision.HIGH

def dot(x, y, precision):
    return jnp.dot(x, y, precision=precision, preferred_element_type=jnp.float32)


def pivot_inverse(pivot, precision):
    order = pivot.shape[0]
    down = lax.broadcasted_iota(jnp.int32, (order, order), 0)
    across = lax.broadcasted_iota(jnp.int32, (order, order), 1)
    eye = (down == across).astype(jnp.float32)
    kept = pivot * eye
    tall = 1.0 / jnp.sqrt(jnp.sum(kept, axis=1, keepdims=True))
    wide = 1.0 / jnp.sqrt(jnp.sum(kept, axis=0, keepdims=True))
    unit = pivot * tall * wide
    ceiling = jnp.max(jnp.sum(jnp.abs(unit), axis=1, keepdims=True), axis=0, keepdims=True)
    power = eye - unit / ceiling
    total = eye + power
    power = dot(power, power, precision)
    for turn in range(1, PIVOT_ITERS - 1):
        both = dot(power, jnp.concatenate([power, total], 1), precision)
        total = total + both[:, order:]
        power = both[:, :order]
    total = total + dot(power, total, precision)
    return total / ceiling * tall * wide


class Plan:
    def __init__(self, mesh):
        self.rows = mesh.shape["row"]
        self.cols = mesh.shape["col"]
        line = list(mesh.devices.reshape(self.rows, self.cols)[0])
        at = [tuple(getattr(device, "coords", (place, 0, 0))) for place, device in enumerate(line)]
        paired = self.cols % 2 == 0 and all(at[2 * i] == at[2 * i + 1] for i in range(self.cols // 2))
        self.cores = 2 if paired else 1
        chips = at[:: self.cores]
        wide = len({chip[0] for chip in chips})
        tall = len({chip[1] for chip in chips})
        low_x, low_y = min(chip[0] for chip in chips), min(chip[1] for chip in chips)
        plane = [(x + low_x, y + low_y) for y in range(tall) for x in range(wide)]
        if [(chip[0], chip[1]) for chip in chips] != plane:
            wide, tall = len(chips), 1
        self.wide, self.tall = wide, tall


SLOTS = 4
WAYS = ((1, 0), (-1, 0), (0, 1), (0, -1))


def unit():
    down = lax.broadcasted_iota(jnp.int32, (PANEL, PANEL), 0)
    across = lax.broadcasted_iota(jnp.int32, (PANEL, PANEL), 1)
    return (down == across).astype(jnp.float32)


def squares(m):
    total = jnp.zeros((8, 128), jnp.float32)
    for j in range(m.shape[0]):
        value = m[j]
        folded = jnp.sum((value * value).reshape(-1, 8, PANEL), axis=0)
        total = total + folded[:, :128] + folded[:, 128:]
    return total


def sweep_kernel(
    plan, steps, wide_a, pieces,
    b_ref, a_ref, c_ref,
    o_ref, sums_ref, ar_ref, cr_ref, ac_ref, ad_ref,
    m, w, r, x, t, in_row, in_col,
    in_sem, row_recv, row_up, row_down, w_recv, w_send, w_pair,
    z_recv, z_send, ac_recv, ac_send, ac_pair, ad_recv, ad_send, ad_pair,
    sum_row_recv, sum_row_send, sum_col_recv, sum_col_send,
):
    tiles, height, _ = m.shape
    blocks = height // PANEL
    half = PANEL // 2
    me_row = lax.axis_index("row")
    me_col = lax.axis_index("col")
    cores = plan.cores
    chip = me_col // cores
    core = me_col % cores
    pair = chip * cores + (cores - 1 - core)
    at_x, at_y = chip % plan.wide, chip // plan.wide

    def to_row(place):
        return {"row": place, "col": me_col}

    def to_col(place):
        return {"row": me_row, "col": place}

    def remote(src, dst, send, recv, target):
        return pltpu.make_async_remote_copy(
            src_ref=src, dst_ref=dst, send_sem=send, recv_sem=recv,
            device_id=target, device_id_type=pl.DeviceIdType.MESH,
        )

    loads = [
        pltpu.make_async_copy(b_ref.at[:, pl.ds(j * PANEL, PANEL)], m.at[j], in_sem.at[j]) for j in range(tiles)
    ]
    for load in loads:
        load.start()

    barrier = pltpu.get_barrier_semaphore()
    for d in range(1, plan.rows):
        pl.semaphore_signal(
            barrier, inc=1, device_id=to_row((me_row + d) % plan.rows), device_id_type=pl.DeviceIdType.MESH
        )
    for d in range(1, plan.cols):
        pl.semaphore_signal(
            barrier, inc=1, device_id=to_col((me_col + d) % plan.cols), device_id_type=pl.DeviceIdType.MESH
        )
    pl.semaphore_wait(barrier, plan.rows + plan.cols - 2)
    for load in loads:
        load.wait()

    def row_root(p):
        return p // blocks

    def col_root(p):
        return p // tiles

    def row_copy(p, i, up):
        part = r.at[p, (p + i) % tiles]
        sem = (row_up if up else row_down).at[p, i]
        return remote(part, part, sem, row_recv.at[p, i], to_row(me_row + 1 if up else me_row - 1))

    def row_sends(p, i, act):
        @pl.when((me_row >= row_root(p)) & (me_row < plan.rows - 1))
        def _():
            act(row_copy(p, i, True))

        @pl.when((me_row <= row_root(p)) & (me_row > 0))
        def _():
            act(row_copy(p, i, False))

    def routes(root, h):
        at = root // cores
        from_x, from_y = at % plan.wide, at // plan.wide
        carry = me_col == root
        if cores == 2:
            carry = carry | ((chip != at) & (core == h))
        else:
            carry = carry | (me_col != root)
        found = []
        for way, (dx, dy) in enumerate(WAYS):
            span, place, origin = (plan.wide, at_x, from_x) if dx else (plan.tall, at_y, from_y)
            if span == 1:
                continue
            on = (place >= origin) & (place < span - 1) if dx + dy > 0 else (place <= origin) & (place > 0)
            if dx and h == 0:
                on = on & (at_y == from_y)
            if dy and h == 1:
                on = on & (at_x == from_x)
            target = (chip + dx + dy * plan.wide) * cores + (h if cores == 2 else 0)
            found.append((way, carry & on, target))
        return carry, found

    def panel_sends(root, h, ref, recv, send, couple, act):
        carry, found = routes(root, h)
        for way, on, target in found:

            @pl.when(on)
            def _():
                act(remote(ref, ref, send(way), recv, to_col(target)))

        if cores == 2:

            @pl.when(carry)
            def _():
                act(remote(ref, ref, couple, recv, to_col(pair)))

    def piece(p, h, i):
        start = ((p + 1 + i) % blocks) * PANEL + h * half
        return w.at[p, pl.ds(pl.multiple_of(start, half), half)]

    def w_sends(p, h, i, act):
        slot = p % SLOTS
        panel_sends(
            col_root(p), h, piece(p, h, i), w_recv.at[p, h, i],
            lambda way: w_send.at[way, slot, h, i], w_pair.at[slot, h, i], act,
        )

    def w_wait(p, h, i):
        remote(piece(p, h, i), piece(p, h, i), w_pair.at[0, 0, 0], w_recv.at[p, h, i], to_col(pair)).wait_recv()

    def start(copy):
        copy.start()

    def sent(copy):
        copy.wait_send()

    def take_carried(p, which):
        @pl.when(me_col != col_root(p))
        def _():
            for i in which:
                for h in range(2):
                    if cores == 2:

                        @pl.when((core == h) & (chip != col_root(p) // cores))
                        def _():
                            w_wait(p, h, i)
                            w_sends(p, h, i, start)

                    else:
                        w_wait(p, h, i)
                        w_sends(p, h, i, start)

    def take_other(p, which):
        if cores == 2:

            @pl.when(me_col != col_root(p))
            def _():
                home = chip == col_root(p) // cores
                for i in which:
                    for h in range(2):

                        @pl.when((core != h) | home)
                        def _():
                            w_wait(p, h, i)

    def drain(p):
        for i in range(blocks):
            for h in range(2):
                w_sends(p, h, i, sent)

    def block(p):
        return pl.ds(pl.multiple_of((p % blocks) * PANEL, PANEL), PANEL)

    def make_rows(p):
        for j in range(tiles):
            fresh = m[j, block(p), :]

            @pl.when(p == 0)
            def _():
                r[p, j] = fresh

            @pl.when(p > 0)
            def _():
                q = jnp.maximum(p - 1, 0)
                step = w[q, block(p), :]
                swept = (me_col == col_root(q)) & (q % tiles == j)

                @pl.when(swept)
                def _():
                    r[p, j] = -step

                @pl.when(jnp.logical_not(swept))
                def _():
                    r[p, j] = fresh - dot(step, r[q, j], SPLIT)

    def make_w(p):
        j = p % tiles

        @pl.when(p == 0)
        def _():
            t[...] = m[j]

        @pl.when(p > 0)
        def _():
            q = jnp.maximum(p - 1, 0)
            t[...] = m[j] - dot(w[q], r[q, j], SPLIT)

        @pl.when(me_row == row_root(p))
        def _():
            t[block(p), :] = t[block(p), :] - unit()

        w[p] = dot(t[...], x[...], SPLIT)

    def update(q):
        for j in range(tiles):
            swept = (me_col == col_root(q)) & (q % tiles == j)

            @pl.when(swept)
            def _():
                m[j] = -w[q]

                @pl.when(me_row == row_root(q))
                def _():
                    m[j, block(q), :] = unit() - w[q, block(q), :]

            @pl.when(jnp.logical_not(swept))
            def _():
                m[j] = m[j] - dot(w[q], r[q, j], SPLIT)

    def z_copy(i, own):
        kind, low, high = pieces[i]
        there = (ar_ref if kind == "a" else cr_ref).at[:, pl.ds(low, high - low)]
        here = (a_ref if kind == "a" else c_ref).at[pl.ds(0, wide_a), pl.ds(low, high - low)] if own else there
        return remote(here, there, z_send.at[i], z_recv.at[i], to_row(jnp.minimum(me_row + 1, plan.rows - 1)))

    def z_turn(p):
        for i in range(len(pieces)):

            @pl.when((p == blocks * (me_row + 1) - 1 + i) & (me_row < plan.rows - 1))
            def _():
                @pl.when(me_row == 0)
                def _():
                    z_copy(i, True).start()

                @pl.when(me_row > 0)
                def _():
                    z_copy(i, False).wait_recv()
                    z_copy(i, False).start()

    def spread_turn(p, first, stride, here, there, recv, send, couple):
        rows = there.shape[0] // 2

        def half_of(ref, h):
            return ref.at[pl.ds(h * rows, rows)]

        def sends(ref, h, act):
            carry, found = routes(jnp.int32(0), h)
            for way, on, target in found:

                @pl.when(on)
                def _():
                    act(remote(half_of(ref, h), half_of(there, h), send.at[way, h], recv.at[h], to_col(target)))

            if cores == 2:

                @pl.when(carry)
                def _():
                    act(remote(half_of(ref, h), half_of(there, h), couple.at[h], recv.at[h], to_col(pair)))

        def wait(h):
            remote(half_of(there, h), half_of(there, h), couple.at[h], recv.at[h], to_col(pair)).wait_recv()

        turn = jnp.minimum(first + stride * (at_x + at_y), steps)

        @pl.when((p == turn) & (me_col == 0))
        def _():
            here(lambda ref: [sends(ref, h, start) for h in range(2)])

        @pl.when((p == turn) & (me_col != 0))
        def _():
            for h in range(2):
                if cores == 2:

                    @pl.when((core == h) & (chip != 0))
                    def _():
                        wait(h)
                        sends(there, h, start)

                else:
                    wait(h)
                    sends(there, h, start)

        def last():
            if cores == 2:

                @pl.when(me_col != 0)
                def _():
                    for h in range(2):

                        @pl.when((core != h) | (chip == 0))
                        def _():
                            wait(h)

            for h in range(2):
                sends(there, h, sent)

        return last

    def own_columns(act):
        act(a_ref.at[:, pl.ds(0, wide_a)])

    def own_top(act):
        @pl.when(me_row == 0)
        def _():
            act(a_ref.at[pl.ds(0, wide_a), pl.ds(0, wide_a)])

        @pl.when(me_row > 0)
        def _():
            act(ar_ref.at[:, pl.ds(0, wide_a)])

    def wait_top(p):
        @pl.when((p == steps - 2) & (me_row == plan.rows - 1) & (me_row > 0))
        def _():
            z_copy(0, False).wait_recv()

    def spread_turns(p):
        one = spread_turn(p, blocks, blocks, own_columns, ac_ref, ac_recv, ac_send, ac_pair)
        wait_top(p)
        two = spread_turn(p, steps - 2, 1, own_top, ad_ref, ad_recv, ad_send, ad_pair)
        return one, two

    b_part = squares(m)

    def step(p, carry):
        root = me_row == row_root(p)
        owner = me_col == col_root(p)
        q = jnp.maximum(p - 1, 0)

        @pl.when(p >= SLOTS)
        def _():
            drain(jnp.maximum(p - SLOTS, 0))

        @pl.when(jnp.logical_not(root))
        def _():
            row_copy(p, 0, True).wait_recv()
            row_sends(p, 0, start)

        @pl.when(root)
        def _():
            @pl.when(p > 0)
            def _():
                take_carried(q, range(1))
                take_other(q, range(1))

            make_rows(p)
            for i in range(tiles):
                row_sends(p, i, start)

        @pl.when(owner)
        def _():
            x[...] = pivot_inverse(r[p, p % tiles], SPLIT)

        @pl.when(p > 0)
        def _():
            @pl.when(jnp.logical_not(root))
            def _():
                take_carried(q, range(1))
                take_other(q, range(1))

            take_carried(q, range(1, blocks))
            take_other(q, range(1, blocks))

        @pl.when(owner)
        def _():
            make_w(p)
            for i in range(blocks):
                for h in range(2):
                    w_sends(p, h, i, start)

        @pl.when(jnp.logical_not(root))
        def _():
            for i in range(1, tiles):
                row_copy(p, i, True).wait_recv()
                row_sends(p, i, start)

        @pl.when(p > 0)
        def _():
            update(q)

        if WITH_A:
            z_turn(p)
            spread_turns(p)
        return carry

    lax.fori_loop(0, steps, step, 0)
    take_carried(steps - 1, range(blocks))
    take_other(steps - 1, range(blocks))
    update(steps - 1)

    stores = [
        pltpu.make_async_copy(m.at[j], o_ref.at[:, pl.ds(j * PANEL, PANEL)], in_sem.at[j]) for j in range(tiles)
    ]
    for store in stores:
        store.start()

    in_row[me_row, 0] = b_part
    in_row[me_row, 1] = squares(m)
    for d in range(1, plan.rows):
        place = in_row.at[me_row]
        remote(place, place, sum_row_send.at[d], sum_row_recv.at[d], to_row((me_row + d) % plan.rows)).start()
    if WITH_A:
        last = spread_turns(jnp.int32(steps))
    for d in range(1, plan.rows):
        place = in_row.at[(me_row + plan.rows - d) % plan.rows]
        remote(place, place, sum_row_send.at[d], sum_row_recv.at[d], to_row((me_row + d) % plan.rows)).wait_recv()
    in_col[me_col] = jnp.sum(in_row[...], axis=0)
    for d in range(1, plan.cols):
        place = in_col.at[me_col]
        remote(place, place, sum_col_send.at[d], sum_col_recv.at[d], to_col((me_col + d) % plan.cols)).start()
    for d in range(1, plan.cols):
        place = in_col.at[(me_col + plan.cols - d) % plan.cols]
        remote(place, place, sum_col_send.at[d], sum_col_recv.at[d], to_col((me_col + d) % plan.cols)).wait_recv()
    sums_ref[...] = jnp.sum(in_col[...], axis=0)

    if WITH_A:
        for finish in last:
            finish()

        @pl.when(me_row < plan.rows - 1)
        def _():
            for i in range(len(pieces)):
                z_copy(i, False).wait_send()

        @pl.when((me_row == plan.rows - 1) & (me_row > 0))
        def _():
            for i in range(1, len(pieces)):
                z_copy(i, False).wait_recv()

    for d in range(1, plan.rows):
        place = in_row.at[me_row]
        remote(place, place, sum_row_send.at[d], sum_row_recv.at[d], to_row((me_row + d) % plan.rows)).wait_send()
    for d in range(1, plan.cols):
        place = in_col.at[me_col]
        remote(place, place, sum_col_send.at[d], sum_col_recv.at[d], to_col((me_col + d) % plan.cols)).wait_send()

    def row_drain(p, carry):
        for i in range(tiles):
            row_sends(p, i, sent)
        return carry

    lax.fori_loop(0, steps, row_drain, 0)
    lax.fori_loop(steps - SLOTS, steps, lambda p, carry: (drain(p), carry)[1], 0)
    for store in stores:
        store.wait()


WITH_A = True


def sweep_b(plan, matrix, a_matrix, c_matrix):
    height, width = matrix.shape
    tiles = width // PANEL
    blocks = height // PANEL
    steps = STEPS_B
    wide_a = STEPS_A * PANEL
    a_cols, c_cols = a_matrix.shape[1], c_matrix.shape[1]
    pieces = [("a", 0, wide_a)]
    if a_cols > wide_a:
        pieces.append(("a", wide_a, a_cols))
    pieces.append(("c", 0, c_cols))
    assert blocks * (plan.rows - 1) + len(pieces) - 2 < steps
    assert wide_a <= min(a_matrix.shape)
    dma = pltpu.SemaphoreType.DMA
    vmem = pltpu.VMEM
    return pl.pallas_call(
        functools.partial(sweep_kernel, plan, steps, wide_a, pieces),
        out_shape=[
            jax.ShapeDtypeStruct((height, width), jnp.float32),
            jax.ShapeDtypeStruct((2, 8, 128), jnp.float32),
            jax.ShapeDtypeStruct((wide_a, a_cols), jnp.float32),
            jax.ShapeDtypeStruct((wide_a, c_cols), jnp.float32),
            jax.ShapeDtypeStruct((a_matrix.shape[0], wide_a), jnp.float32),
            jax.ShapeDtypeStruct((wide_a, wide_a), jnp.float32),
        ],
        in_specs=[pl.BlockSpec(memory_space=pl.ANY)] * 3,
        out_specs=[
            pl.BlockSpec(memory_space=pl.ANY),
            pl.BlockSpec(memory_space=pltpu.VMEM),
        ]
        + [pl.BlockSpec(memory_space=pl.ANY)] * 4,
        scratch_shapes=[
            vmem((tiles, height, PANEL), jnp.float32),
            vmem((steps, height, PANEL), jnp.float32),
            vmem((steps, tiles, PANEL, PANEL), jnp.float32),
            vmem((PANEL, PANEL), jnp.float32),
            vmem((height, PANEL), jnp.float32),
            vmem((plan.rows, 2, 8, 128), jnp.float32),
            vmem((plan.cols, 2, 8, 128), jnp.float32),
            dma((tiles,)),
            dma((steps, tiles)),
            dma((steps, tiles)),
            dma((steps, tiles)),
            dma((steps, 2, blocks)),
            dma((4, SLOTS, 2, blocks)),
            dma((SLOTS, 2, blocks)),
            dma((len(pieces),)),
            dma((len(pieces),)),
            dma((2,)),
            dma((4, 2)),
            dma((2,)),
            dma((2,)),
            dma((4, 2)),
            dma((2,)),
            dma((plan.rows,)),
            dma((plan.rows,)),
            dma((plan.cols,)),
            dma((plan.cols,)),
        ],
        compiler_params=pltpu.CompilerParams(
            collective_id=0, has_side_effects=True, vmem_limit_bytes=56 * 1024 * 1024
        ),
        name="sweep_b",
    )(matrix, a_matrix, c_matrix)


def finish_kernel(
    wide_a, tile, a_any, c_any, ar_any, cr_any, ac_any, ad_any, a_blk, c_blk, ao_blk, co_blk,
    col, rows, top, w, sem,
):
    me_row = lax.axis_index("row")
    me_col = lax.axis_index("col")
    a_cols = a_blk.shape[1]
    count = wide_a // PANEL
    here = pl.program_id(0)

    def part(s):
        return pl.ds(s * PANEL, PANEL)

    @pl.when(here == 0)
    def _():
        top_row, left = me_row == 0, me_col == 0

        def fetch(on, src, dst, i):
            @pl.when(on)
            def _():
                pltpu.make_async_copy(src, dst, sem.at[i]).start()

        def fetched(dst, i):
            pltpu.make_async_copy(dst, dst, sem.at[i]).wait()

        first = pl.ds(0, wide_a)
        a_part = rows.at[:, pl.ds(0, a_cols)]
        c_part = rows.at[:, pl.ds(a_cols, rows.shape[1] - a_cols)]
        fetch(left & top_row, a_any.at[first, first], top, 0)
        fetch(left & jnp.logical_not(top_row), ar_any.at[:, first], top, 0)
        fetch(jnp.logical_not(left), ad_any, top, 0)
        fetch(left, a_any.at[:, first], col, 1)
        fetch(jnp.logical_not(left), ac_any, col, 1)
        fetch(top_row, a_any.at[first], a_part, 2)
        fetch(jnp.logical_not(top_row), ar_any, a_part, 2)
        fetch(top_row, c_any.at[first], c_part, 3)
        fetch(jnp.logical_not(top_row), cr_any, c_part, 3)
        for i, dst in enumerate((top, col, a_part, c_part)):
            fetched(dst, i)

        for s in range(count):
            inverse = pivot_inverse(top[part(s), part(s)], SPLIT)
            top[part(s), part(s)] = top[part(s), part(s)] - unit()

            @pl.when(top_row)
            def _():
                col[part(s), part(s)] = col[part(s), part(s)] - unit()

            w[:, part(s)] = dot(col[:, part(s)], inverse, SPLIT)

            @pl.when(left)
            def _():
                rows[:, part(s)] = jnp.zeros((wide_a, PANEL), jnp.float32)
                rows[part(s), part(s)] = unit()

            for later in range(s + 1, count):
                near = dot(top[part(later), part(s)], inverse, SPLIT)
                rows[part(later), :] = rows[part(later), :] - dot(near, rows[part(s), :], SPLIT)
                col[:, part(later)] = col[:, part(later)] - dot(w[:, part(s)], top[part(s), part(later)], SPLIT)
                for after in range(s + 1, count):
                    top[part(later), part(after)] = top[part(later), part(after)] - dot(
                        near, top[part(s), part(after)], SPLIT
                    )

    mine = pl.ds(pl.multiple_of(here * tile, tile), tile)
    taken = dot(w[mine, :], rows[...], SPLIT)
    ao_blk[...] = a_blk[...] - taken[:, :a_cols]
    co_blk[...] = c_blk[...] - taken[:, a_cols:]

    @pl.when(me_col == 0)
    def _():
        down = lax.broadcasted_iota(jnp.int32, (tile, wide_a), 0) + here * tile + me_row * a_any.shape[0]
        across = lax.broadcasted_iota(jnp.int32, (tile, wide_a), 1)
        ao_blk[:, :wide_a] = (down == across).astype(jnp.float32) - taken[:, :wide_a]


def finish_a(a_matrix, c_matrix, a_rows, c_rows, a_cols, a_top):
    height, width = a_matrix.shape
    c_width = c_matrix.shape[1]
    wide_a = a_cols.shape[1]
    tile = PANEL
    return pl.pallas_call(
        functools.partial(finish_kernel, wide_a, tile),
        grid=(height // tile,),
        out_shape=[
            jax.ShapeDtypeStruct((height, width), jnp.float32),
            jax.ShapeDtypeStruct((height, c_width), jnp.float32),
        ],
        in_specs=[pl.BlockSpec(memory_space=pl.ANY)] * 6
        + [pl.BlockSpec((tile, width), lambda i: (i, 0)), pl.BlockSpec((tile, c_width), lambda i: (i, 0))],
        out_specs=[pl.BlockSpec((tile, width), lambda i: (i, 0)), pl.BlockSpec((tile, c_width), lambda i: (i, 0))],
        scratch_shapes=[
            pltpu.VMEM((height, wide_a), jnp.float32),
            pltpu.VMEM((wide_a, width + c_width), jnp.float32),
            pltpu.VMEM((wide_a, wide_a), jnp.float32),
            pltpu.VMEM((height, wide_a), jnp.float32),
            pltpu.SemaphoreType.DMA((4,)),
        ],
        compiler_params=pltpu.CompilerParams(vmem_limit_bytes=48 * 1024 * 1024),
        name="finish_a",
    )(a_matrix, c_matrix, a_rows, c_rows, a_cols, a_top, a_matrix, c_matrix)


def body(plan, a_matrix, b_matrix, c_matrix):
    b_inverse, sums, a_rows, c_rows, a_cols, a_top = sweep_b(plan, b_matrix, a_matrix, c_matrix)
    a_swept, c_swept = finish_a(a_matrix, c_matrix, a_rows, c_rows, a_cols, a_top)
    b_squares, inv_squares = jnp.sum(sums[0]), jnp.sum(sums[1])
    scale = jnp.sqrt(jnp.sqrt(inv_squares / b_squares))
    b_next = 0.5 * (scale * b_matrix + b_inverse / scale)
    return (a_swept, c_swept, b_next)


def solution(mesh):
    return jax.shard_map(
        functools.partial(body, Plan(mesh)),
        mesh=mesh,
        in_specs=(P("row", "col"), P("row", "col"), P("row", "col")),
        out_specs=(P("row", "col"), P("row", "col"), P("row", "col")),
        check_vma=False,
    )
```

profile of v0, /device:TPU:15, one launch (start us, length us, event | category | flops | bytes accessed | tf_op | source)
XLA Modules:
  0.0 361.6 jit_solution(4777778617474925774)
XLA Ops:
  0.6 0.0 copy-start.3
  0.6 327.4 %sweep_b.1 = (f32[1024,512]{1,0:T(8,128)}, f32[2,8,128]{2,1,0:T(8,128)}, f32[512,1024]{1,0:T(8,128)}, f32[512,512]{1,0:T(8,128)}, f32[2048,512]{1,0:T(8,128)}, /*index=5*/f32[512,512]{1,0:T(8,128)}) custom-call(f32[1024,512]{1,0:T(8,128)} %b_ref.1, f32[2048,1024]{1,0:T(8,128)} %a_blk.1, f32[2048,512]{1,0:T(8,128)} %c_blk.1), custom_call_target="tpu_custom_call" | custom-call | tf_op jit(solution)/shard_map/sweep_b/pallas_call | solution.py:545
  328.0 1.3 slice_reduce_fusion
  330.8 0.0 copy-done.3
  330.8 0.0 copy-start
  330.8 0.0 copy-start.1
  330.8 0.0 copy-start.2
  330.8 3.6 add_multiply_fusion
  334.4 0.0 copy-done
  334.4 0.0 copy-done.1
  334.4 0.0 copy-done.2
  334.4 27.0 %finish_a.1 = (f32[2048,1024]{1,0:T(8,128)}, f32[2048,512]{1,0:T(8,128)}) custom-call(f32[2048,1024]{1,0:T(8,128)} %a_blk.1, f32[2048,512]{1,0:T(8,128)} %c_blk.1, f32[512,1024]{1,0:T(8,128)S(1)} %copy-done, f32[512,512]{1,0:T(8,128)S(1)} %copy-done.1, f32[2048,512]{1,0:T(8,128)} %get-tuple-element.13.ac_any, f32[512,512]{1,0:T(8,128)S(1)} %copy-done.2, ...), custom_call_target="tpu_custom_call" | custom-call | tf_op jit(solution)/shard_map/finish_a/pallas_call | solution.py:677
Async XLA Ops:
  0.6 330.1 %copy-start.3 = (f32[1024,512]{1,0:T(8,128)S(1)}, f32[1024,512]{1,0:T(8,128)}, u32[]{:S(2)}) copy-start(f32[1024,512]{1,0:T(8,128)} %b_ref.1) | copy-start | bytes 6291460
  330.8 3.6 %copy-start = (f32[512,1024]{1,0:T(8,128)S(1)}, f32[512,1024]{1,0:T(8,128)}, u32[]{:S(2)}) copy-start(f32[512,1024]{1,0:T(8,128)} %get-tuple-element.11.ar_any) | copy-start | bytes 6291460
  330.8 3.6 %copy-start.1 = (f32[512,512]{1,0:T(8,128)S(1)}, f32[512,512]{1,0:T(8,128)}, u32[]{:S(2)}) copy-start(f32[512,512]{1,0:T(8,128)} %get-tuple-element.12.cr_any) | copy-start | bytes 3145732
  330.8 3.6 copy-start.2
where the time goes:
time: 362 us
  Pallas kernels  354 us (98%)
  other arithmetic  4.88 us (1%)
    pallas_call x1, Pallas kernels, sweep_b(): pl.pallas_call(functools.partial(sweep_kernel, plan, steps, wide_a, piece...  327 us
    pallas_call x1, Pallas kernels, finish_a(): pl.pallas_call(functools.partial(finish_kernel, wide_a, tile), grid=(heig...  27 us

commit v1 on v0

--- a/solution.py
+++ b/solution.py
@@ -80,15 +80,16 @@
 def sweep_kernel(
     plan, steps, wide_a, pieces,
     b_ref, a_ref, c_ref,
-    o_ref, sums_ref, ar_ref, cr_ref, ac_ref, ad_ref,
+    o_ref, sums_ref, ar_ref, cr_ref, ac_ref,
     m, w, r, x, t, in_row, in_col,
     in_sem, row_recv, row_up, row_down, w_recv, w_send, w_pair,
-    z_recv, z_send, ac_recv, ac_send, ac_pair, ad_recv, ad_send, ad_pair,
+    z_recv, z_send, ac_recv, ac_send, ac_pair,
     sum_row_recv, sum_row_send, sum_col_recv, sum_col_send,
 ):
     tiles, height, _ = m.shape
     blocks = height // PANEL
-    half = PANEL // 2
+    square = plan.wide == 2 and plan.tall == 2
+    kinds = ("xy", "yx")
     me_row = lax.axis_index("row")
     me_col = lax.axis_index("col")
     cores = plan.cores
@@ -148,7 +149,7 @@
         def _():
             act(row_copy(p, i, False))
 
-    def routes(root, h):
+    def routes(root, kind, h):
         at = root // cores
         from_x, from_y = at % plan.wide, at // plan.wide
         carry = me_col == root
@@ -156,47 +157,58 @@
             carry = carry | ((chip != at) & (core == h))
         else:
             carry = carry | (me_col != root)
+        aside, apart = at_x != from_x, at_y != from_y
         found = []
         for way, (dx, dy) in enumerate(WAYS):
             span, place, origin = (plan.wide, at_x, from_x) if dx else (plan.tall, at_y, from_y)
             if span == 1:
                 continue
-            on = (place >= origin) & (place < span - 1) if dx + dy > 0 else (place <= origin) & (place > 0)
-            if dx and h == 0:
-                on = on & (at_y == from_y)
-            if dy and h == 1:
-                on = on & (at_x == from_x)
+            if kind in ("xy", "yx"):
+                on = (place >= origin) & (place < span - 1) if dx + dy > 0 else (place <= origin) & (place > 0)
+                if dx and kind == "xy":
+                    on = on & jnp.logical_not(apart)
+                if dy and kind == "yx":
+                    on = on & jnp.logical_not(aside)
+            else:
+                on = place < span - 1 if dx + dy > 0 else place > 0
+                same = aside == apart
+                if kind == "ring x":
+                    on = on & (same if dx else aside & jnp.logical_not(apart))
+                else:
+                    on = on & (same if dy else apart & jnp.logical_not(aside))
             target = (chip + dx + dy * plan.wide) * cores + (h if cores == 2 else 0)
             found.append((way, carry & on, target))
         return carry, found
 
-    def panel_sends(root, h, ref, recv, send, couple, act):
-        carry, found = routes(root, h)
+    def panel_sends(root, kind, h, src, dst, recv, send, couple, act, ways=(0, 1, 2, 3), across=True):
+        carry, found = routes(root, kind, h)
         for way, on, target in found:
+            if way not in ways:
+                continue
 
             @pl.when(on)
             def _():
-                act(remote(ref, ref, send(way), recv, to_col(target)))
-
-        if cores == 2:
+                act(remote(src, dst, send(way), recv, to_col(target)))
+
+        if cores == 2 and across:
 
             @pl.when(carry)
             def _():
-                act(remote(ref, ref, couple, recv, to_col(pair)))
-
-    def piece(p, h, i):
-        start = ((p + 1 + i) % blocks) * PANEL + h * half
-        return w.at[p, pl.ds(pl.multiple_of(start, half), half)]
-
-    def w_sends(p, h, i, act):
+                act(remote(src, dst, couple, recv, to_col(pair)))
+
+    def piece(p, i):
+        return w.at[p, pl.ds(pl.multiple_of(((p + 1 + i) % blocks) * PANEL, PANEL), PANEL)]
+
+    def w_sends(p, i, act, **which):
         slot = p % SLOTS
+        part = piece(p, i)
         panel_sends(
-            col_root(p), h, piece(p, h, i), w_recv.at[p, h, i],
-            lambda way: w_send.at[way, slot, h, i], w_pair.at[slot, h, i], act,
+            col_root(p), kinds[i % len(kinds)], i % 2, part, part, w_recv.at[p, i],
+            lambda way: w_send.at[way, slot, i], w_pair.at[slot, i], act, **which,
         )
 
-    def w_wait(p, h, i):
-        remote(piece(p, h, i), piece(p, h, i), w_pair.at[0, 0, 0], w_recv.at[p, h, i], to_col(pair)).wait_recv()
+    def w_wait(p, i):
+        remote(piece(p, i), piece(p, i), w_pair.at[0, 0], w_recv.at[p, i], to_col(pair)).wait_recv()
 
     def start(copy):
         copy.start()
@@ -204,39 +216,35 @@
     def sent(copy):
         copy.wait_send()
 
-    def take_carried(p, which):
+    def take(p, which):
         @pl.when(me_col != col_root(p))
         def _():
-            for i in which:
-                for h in range(2):
-                    if cores == 2:
-
-                        @pl.when((core == h) & (chip != col_root(p) // cores))
-                        def _():
-                            w_wait(p, h, i)
-                            w_sends(p, h, i, start)
-
-                    else:
-                        w_wait(p, h, i)
-                        w_sends(p, h, i, start)
-
-    def take_other(p, which):
-        if cores == 2:
-
-            @pl.when(me_col != col_root(p))
-            def _():
-                home = chip == col_root(p) // cores
+            home = chip == col_root(p) // cores
+            if cores == 1:
                 for i in which:
-                    for h in range(2):
-
-                        @pl.when((core != h) | home)
-                        def _():
-                            w_wait(p, h, i)
+                    w_wait(p, i)
+                    w_sends(p, i, start)
+                return
+            for h in range(2):
+
+                @pl.when(jnp.logical_not(home) & (core == h))
+                def _():
+                    for i in which:
+                        if i % 2 == h:
+                            w_wait(p, i)
+                            w_sends(p, i, start)
+                    for i in which:
+                        if i % 2 != h:
+                            w_wait(p, i)
+
+            @pl.when(home)
+            def _():
+                for i in which:
+                    w_wait(p, i)
 
     def drain(p):
         for i in range(blocks):
-            for h in range(2):
-                w_sends(p, h, i, sent)
+            w_sends(p, i, sent)
 
     def block(p):
         return pl.ds(pl.multiple_of((p % blocks) * PANEL, PANEL), PANEL)
@@ -317,87 +325,118 @@
                     z_copy(i, False).wait_recv()
                     z_copy(i, False).start()
 
-    def spread_turn(p, first, stride, here, there, recv, send, couple):
-        rows = there.shape[0] // 2
-
-        def half_of(ref, h):
-            return ref.at[pl.ds(h * rows, rows)]
-
-        def sends(ref, h, act):
-            carry, found = routes(jnp.int32(0), h)
-            for way, on, target in found:
-
-                @pl.when(on)
+    half = PANEL // 2
+    top_parts = wide_a // PANEL
+    top_turn = steps - 1 - top_parts
+    tall_half = a_ref.shape[0] // 2
+    first = pl.ds(0, wide_a)
+
+    def a_there(c, h):
+        if isinstance(c, int) and c == 0:
+            return ac_ref.at[pl.ds(h * tall_half, tall_half)]
+        return ac_ref.at[pl.ds(pl.multiple_of(2 * tall_half + (c - 1) * PANEL + h * half, half), half)]
+
+    def a_own(c, h, act):
+        if isinstance(c, int) and c == 0:
+            act(a_ref.at[pl.ds(h * tall_half, tall_half), first])
+            return
+        spot = pl.ds(pl.multiple_of((c - 1) * PANEL + h * half, half), half)
+
+        @pl.when(me_row == 0)
+        def _():
+            act(a_ref.at[spot, first])
+
+        @pl.when(me_row > 0)
+        def _():
+            act(ar_ref.at[spot, first])
+
+    def a_sends(c, h, src, act, **which):
+        kind = "xy" if isinstance(c, int) and c == 0 else ("xy", "yx")[h]
+        panel_sends(
+            jnp.int32(0), kind, h, src, a_there(c, h), ac_recv.at[c, h],
+            lambda way: ac_send.at[way, c, h], ac_pair.at[c, h], act, **which,
+        )
+
+    def a_wait(c, h):
+        part = a_there(c, h)
+        remote(part, part, ac_pair.at[c, h], ac_recv.at[c, h], to_col(pair)).wait_recv()
+
+    def a_carries(h):
+        return (chip != 0) & ((core == h) | (cores == 1))
+
+    def a_pass(c, h):
+        @pl.when(me_col == 0)
+        def _():
+            a_own(c, h, lambda ref: a_sends(c, h, ref, start))
+
+        @pl.when(a_carries(h))
+        def _():
+            a_wait(c, h)
+            a_sends(c, h, a_there(c, h), start)
+
+    col_turn = jnp.where(
+        at_y == 0, 2 * blocks + 2 * (at_x - 1), 3 * blocks + 2 * at_x + 2 * (at_y - 1)
+    )
+
+    def col_start(p):
+        for h in range(2):
+
+            @pl.when((me_col == 0) & (p == blocks))
+            def _():
+                a_own(0, h, lambda ref: a_sends(0, h, ref, start, ways=(0, 1)))
+
+            @pl.when((me_col == 0) & (p == 2 * blocks))
+            def _():
+                a_own(0, h, lambda ref: a_sends(0, h, ref, start, ways=(2, 3), across=False))
+
+    def col_pass(on):
+        for h in range(2):
+
+            @pl.when(a_carries(h) & on)
+            def _():
+                a_wait(0, h)
+                a_sends(0, h, a_there(0, h), start)
+
+    def wait_top():
+        @pl.when((me_row == plan.rows - 1) & (me_row > 0))
+        def _():
+            z_copy(0, False).wait_recv()
+
+    def a_turn(p):
+        col_start(p)
+        col_pass(p == col_turn)
+
+        @pl.when(p == top_turn)
+        def _():
+            wait_top()
+
+        for h in range(2):
+            c = p - top_turn - at_x - at_y
+
+            @pl.when((c >= 0) & (c < top_parts))
+            def _():
+                a_pass(1 + jnp.clip(c, 0, top_parts - 1), h)
+
+    def a_last():
+        col_pass(col_turn >= steps)
+        for c in range(top_parts):
+            for h in range(2):
+
+                @pl.when(top_turn + c + at_x + at_y >= steps)
                 def _():
-                    act(remote(half_of(ref, h), half_of(there, h), send.at[way, h], recv.at[h], to_col(target)))
-
-            if cores == 2:
-
-                @pl.when(carry)
+                    a_pass(1 + c, h)
+
+        if cores == 2:
+            for h in range(2):
+
+                @pl.when((me_col != 0) & ((core != h) | (chip == 0)))
                 def _():
-                    act(remote(half_of(ref, h), half_of(there, h), couple.at[h], recv.at[h], to_col(pair)))
-
-        def wait(h):
-            remote(half_of(there, h), half_of(there, h), couple.at[h], recv.at[h], to_col(pair)).wait_recv()
-
-        turn = jnp.minimum(first + stride * (at_x + at_y), steps)
-
-        @pl.when((p == turn) & (me_col == 0))
-        def _():
-            here(lambda ref: [sends(ref, h, start) for h in range(2)])
-
-        @pl.when((p == turn) & (me_col != 0))
-        def _():
+                    for c in range(1 + top_parts):
+                        a_wait(c, h)
+
+        for c in range(1 + top_parts):
             for h in range(2):
-                if cores == 2:
-
-                    @pl.when((core == h) & (chip != 0))
-                    def _():
-                        wait(h)
-                        sends(there, h, start)
-
-                else:
-                    wait(h)
-                    sends(there, h, start)
-
-        def last():
-            if cores == 2:
-
-                @pl.when(me_col != 0)
-                def _():
-                    for h in range(2):
-
-                        @pl.when((core != h) | (chip == 0))
-                        def _():
-                            wait(h)
-
-            for h in range(2):
-                sends(there, h, sent)
-
-        return last
-
-    def own_columns(act):
-        act(a_ref.at[:, pl.ds(0, wide_a)])
-
-    def own_top(act):
-        @pl.when(me_row == 0)
-        def _():
-            act(a_ref.at[pl.ds(0, wide_a), pl.ds(0, wide_a)])
-
-        @pl.when(me_row > 0)
-        def _():
-            act(ar_ref.at[:, pl.ds(0, wide_a)])
-
-    def wait_top(p):
-        @pl.when((p == steps - 2) & (me_row == plan.rows - 1) & (me_row > 0))
-        def _():
-            z_copy(0, False).wait_recv()
-
-    def spread_turns(p):
-        one = spread_turn(p, blocks, blocks, own_columns, ac_ref, ac_recv, ac_send, ac_pair)
-        wait_top(p)
-        two = spread_turn(p, steps - 2, 1, own_top, ad_ref, ad_recv, ad_send, ad_pair)
-        return one, two
+                a_sends(c, h, a_there(c, h), sent)
 
     b_part = squares(m)
 
@@ -410,8 +449,14 @@
         def _():
             drain(jnp.maximum(p - SLOTS, 0))
 
+        early = blocks
+
         @pl.when(jnp.logical_not(root))
         def _():
+            @pl.when(p > 0)
+            def _():
+                take(q, range(early))
+
             row_copy(p, 0, True).wait_recv()
             row_sends(p, 0, start)
 
@@ -419,8 +464,7 @@
         def _():
             @pl.when(p > 0)
             def _():
-                take_carried(q, range(1))
-                take_other(q, range(1))
+                take(q, range(1))
 
             make_rows(p)
             for i in range(tiles):
@@ -432,20 +476,19 @@
 
         @pl.when(p > 0)
         def _():
-            @pl.when(jnp.logical_not(root))
-            def _():
-                take_carried(q, range(1))
-                take_other(q, range(1))
-
-            take_carried(q, range(1, blocks))
-            take_other(q, range(1, blocks))
+            @pl.when(root)
+            def _():
+                take(q, range(1, early))
+
+            take(q, range(early, blocks))
 
         @pl.when(owner)
         def _():
             make_w(p)
             for i in range(blocks):
-                for h in range(2):
-                    w_sends(p, h, i, start)
+                w_sends(p, i, start, ways=())
+            for i in range(blocks):
+                w_sends(p, i, start, across=False)
 
         @pl.when(jnp.logical_not(root))
         def _():
@@ -459,12 +502,11 @@
 
         if WITH_A:
             z_turn(p)
-            spread_turns(p)
+            a_turn(p)
         return carry
 
     lax.fori_loop(0, steps, step, 0)
-    take_carried(steps - 1, range(blocks))
-    take_other(steps - 1, range(blocks))
+    take(steps - 1, range(blocks))
     update(steps - 1)
 
     stores = [
@@ -478,8 +520,6 @@
     for d in range(1, plan.rows):
         place = in_row.at[me_row]
         remote(place, place, sum_row_send.at[d], sum_row_recv.at[d], to_row((me_row + d) % plan.rows)).start()
-    if WITH_A:
-        last = spread_turns(jnp.int32(steps))
     for d in range(1, plan.rows):
         place = in_row.at[(me_row + plan.rows - d) % plan.rows]
         remote(place, place, sum_row_send.at[d], sum_row_recv.at[d], to_row((me_row + d) % plan.rows)).wait_recv()
@@ -493,8 +533,7 @@
     sums_ref[...] = jnp.sum(in_col[...], axis=0)
 
     if WITH_A:
-        for finish in last:
-            finish()
+        a_last()
 
         @pl.when(me_row < plan.rows - 1)
         def _():
@@ -541,6 +580,7 @@
     assert blocks * (plan.rows - 1) + len(pieces) - 2 < steps
     assert wide_a <= min(a_matrix.shape)
     dma = pltpu.SemaphoreType.DMA
+    parts = 1 + wide_a // PANEL
     vmem = pltpu.VMEM
     return pl.pallas_call(
         functools.partial(sweep_kernel, plan, steps, wide_a, pieces),
@@ -549,15 +589,14 @@
             jax.ShapeDtypeStruct((2, 8, 128), jnp.float32),
             jax.ShapeDtypeStruct((wide_a, a_cols), jnp.float32),
             jax.ShapeDtypeStruct((wide_a, c_cols), jnp.float32),
-            jax.ShapeDtypeStruct((a_matrix.shape[0], wide_a), jnp.float32),
-            jax.ShapeDtypeStruct((wide_a, wide_a), jnp.float32),
+            jax.ShapeDtypeStruct((a_matrix.shape[0] + wide_a, wide_a), jnp.float32),
         ],
         in_specs=[pl.BlockSpec(memory_space=pl.ANY)] * 3,
         out_specs=[
             pl.BlockSpec(memory_space=pl.ANY),
             pl.BlockSpec(memory_space=pltpu.VMEM),
         ]
-        + [pl.BlockSpec(memory_space=pl.ANY)] * 4,
+        + [pl.BlockSpec(memory_space=pl.ANY)] * 3,
         scratch_shapes=[
             vmem((tiles, height, PANEL), jnp.float32),
             vmem((steps, height, PANEL), jnp.float32),
@@ -570,17 +609,14 @@
             dma((steps, tiles)),
             dma((steps, tiles)),
             dma((steps, tiles)),
-            dma((steps, 2, blocks)),
-            dma((4, SLOTS, 2, blocks)),
-            dma((SLOTS, 2, blocks)),
+            dma((steps, blocks)),
+            dma((4, SLOTS, blocks)),
+            dma((SLOTS, blocks)),
             dma((len(pieces),)),
             dma((len(pieces),)),
-            dma((2,)),
-            dma((4, 2)),
-            dma((2,)),
-            dma((2,)),
-            dma((4, 2)),
-            dma((2,)),
+            dma((parts, 2)),
+            dma((4, parts, 2)),
+            dma((parts, 2)),
             dma((plan.rows,)),
             dma((plan.rows,)),
             dma((plan.cols,)),
@@ -593,9 +629,14 @@
     )(matrix, a_matrix, c_matrix)
 
 
+def halves(value):
+    high = value.astype(jnp.bfloat16)
+    return high, (value - high.astype(jnp.float32)).astype(jnp.bfloat16)
+
+
 def finish_kernel(
-    wide_a, tile, a_any, c_any, ar_any, cr_any, ac_any, ad_any, a_blk, c_blk, ao_blk, co_blk,
-    col, rows, top, w, sem,
+    wide_a, tile, a_any, c_any, ar_any, cr_any, ac_any, a_blk, c_blk, ao_blk, co_blk,
+    col, rows, top, w, rows3, w3, sem,
 ):
     me_row = lax.axis_index("row")
     me_col = lax.axis_index("col")
@@ -623,9 +664,9 @@
         c_part = rows.at[:, pl.ds(a_cols, rows.shape[1] - a_cols)]
         fetch(left & top_row, a_any.at[first, first], top, 0)
         fetch(left & jnp.logical_not(top_row), ar_any.at[:, first], top, 0)
-        fetch(jnp.logical_not(left), ad_any, top, 0)
+        fetch(jnp.logical_not(left), ac_any.at[pl.ds(a_any.shape[0], wide_a)], top, 0)
         fetch(left, a_any.at[:, first], col, 1)
-        fetch(jnp.logical_not(left), ac_any, col, 1)
+        fetch(jnp.logical_not(left), ac_any.at[pl.ds(0, a_any.shape[0])], col, 1)
         fetch(top_row, a_any.at[first], a_part, 2)
         fetch(jnp.logical_not(top_row), ar_any, a_part, 2)
         fetch(top_row, c_any.at[first], c_part, 3)
@@ -657,8 +698,13 @@
                         near, top[part(s), part(after)], SPLIT
                     )
 
+        high, low = halves(rows[...])
+        rows3[:wide_a], rows3[wide_a : 2 * wide_a], rows3[2 * wide_a :] = high, low, high
+        high, low = halves(w[...])
+        w3[:, :wide_a], w3[:, wide_a : 2 * wide_a], w3[:, 2 * wide_a :] = high, high, low
+
     mine = pl.ds(pl.multiple_of(here * tile, tile), tile)
-    taken = dot(w[mine, :], rows[...], SPLIT)
+    taken = jnp.dot(w3[mine, :], rows3[...], preferred_element_type=jnp.float32)
     ao_blk[...] = a_blk[...] - taken[:, :a_cols]
     co_blk[...] = c_blk[...] - taken[:, a_cols:]
 
@@ -669,7 +715,7 @@
         ao_blk[:, :wide_a] = (down == across).astype(jnp.float32) - taken[:, :wide_a]
 
 
-def finish_a(a_matrix, c_matrix, a_rows, c_rows, a_cols, a_top):
+def finish_a(a_matrix, c_matrix, a_rows, c_rows, a_cols):
     height, width = a_matrix.shape
     c_width = c_matrix.shape[1]
     wide_a = a_cols.shape[1]
@@ -681,7 +727,7 @@
             jax.ShapeDtypeStruct((height, width), jnp.float32),
             jax.ShapeDtypeStruct((height, c_width), jnp.float32),
         ],
-        in_specs=[pl.BlockSpec(memory_space=pl.ANY)] * 6
+        in_specs=[pl.BlockSpec(memory_space=pl.ANY)] * 5
         + [pl.BlockSpec((tile, width), lambda i: (i, 0)), pl.BlockSpec((tile, c_width), lambda i: (i, 0))],
         out_specs=[pl.BlockSpec((tile, width), lambda i: (i, 0)), pl.BlockSpec((tile, c_width), lambda i: (i, 0))],
         scratch_shapes=[
@@ -689,16 +735,18 @@
             pltpu.VMEM((wide_a, width + c_width), jnp.float32),
             pltpu.VMEM((wide_a, wide_a), jnp.float32),
             pltpu.VMEM((height, wide_a), jnp.float32),
+            pltpu.VMEM((3 * wide_a, width + c_width), jnp.bfloat16),
+            pltpu.VMEM((height, 3 * wide_a), jnp.bfloat16),
             pltpu.SemaphoreType.DMA((4,)),
         ],
         compiler_params=pltpu.CompilerParams(vmem_limit_bytes=48 * 1024 * 1024),
         name="finish_a",
-    )(a_matrix, c_matrix, a_rows, c_rows, a_cols, a_top, a_matrix, c_matrix)
+    )(a_matrix, c_matrix, a_rows, c_rows, a_cols, a_matrix, c_matrix)
 
 
 def body(plan, a_matrix, b_matrix, c_matrix):
-    b_inverse, sums, a_rows, c_rows, a_cols, a_top = sweep_b(plan, b_matrix, a_matrix, c_matrix)
-    a_swept, c_swept = finish_a(a_matrix, c_matrix, a_rows, c_rows, a_cols, a_top)
+    b_inverse, sums, a_rows, c_rows, a_cols = sweep_b(plan, b_matrix, a_matrix, c_matrix)
+    a_swept, c_swept = finish_a(a_matrix, c_matrix, a_rows, c_rows, a_cols)
     b_squares, inv_squares = jnp.sum(sums[0]), jnp.sum(sums[1])
     scale = jnp.sqrt(jnp.sqrt(inv_squares / b_squares))
     b_next = 0.5 * (scale * b_matrix + b_inverse / scale)

time: 362 us -> 324 us (0.90)
  Pallas kernels: 354 us -> 317 us
    pallas_call x1, Pallas kernels: 327 us -> 289 us  [sweep_b(): pl.pallas_call(functools.partial(sweep_kernel, plan, steps, wide_a, piece...]
where the time goes in v1:
time: 324 us
  Pallas kernels  317 us (98%)
  other arithmetic  4.88 us (2%)
    pallas_call x1, Pallas kernels, sweep_b(): pl.pallas_call(functools.partial(sweep_kernel, plan, steps, wide_a, piece...  289 us
    pallas_call x1, Pallas kernels, finish_a(): pl.pallas_call(functools.partial(finish_kernel, wide_a, tile), grid=(heig...  28.1 us

profile of v1, /device:TPU:15, one launch (start us, length us, event | category | flops | bytes accessed | tf_op | source)
XLA Modules:
  0.0 323.9 jit_solution(5782053927831326366)
XLA Ops:
  0.6 0.0 copy-start.2
  0.6 288.6 %sweep_b.1 = (f32[1024,512]{1,0:T(8,128)}, f32[2,8,128]{2,1,0:T(8,128)}, f32[512,1024]{1,0:T(8,128)}, f32[512,512]{1,0:T(8,128)}, f32[2560,512]{1,0:T(8,128)}) custom-call(f32[1024,512]{1,0:T(8,128)} %b_ref.1, f32[2048,1024]{1,0:T(8,128)} %a_blk.1, f32[2048,512]{1,0:T(8,128)} %c_blk.1), custom_call_target="tpu_custom_call" | custom-call | tf_op jit(solution)/shard_map/sweep_b/pallas_call | solution.py:585
  289.2 1.3 slice_reduce_fusion
  292.0 0.0 copy-done.2
  292.0 0.0 copy-start
  292.0 0.0 copy-start.1
  292.0 3.6 %add_multiply_fusion = f32[1024,512]{1,0:T(8,128)} fusion(f32[1024,512]{1,0:T(8,128)} %get-tuple-element.16, f32[1024,512]{1,0:T(8,128)S(1)} %copy-done.2, f32[]{:T(128)S(6)} %sqrt.7), kind=kLoop, calls=%fused_computation | loop fusion | flops 2097152 | bytes 6291460 | tf_op jit(solution)/shard_map/mul | solution.py:752
  295.6 0.0 copy-done
  295.6 0.0 copy-done.1
  295.6 28.1 %finish_a.1 = (f32[2048,1024]{1,0:T(8,128)}, f32[2048,512]{1,0:T(8,128)}) custom-call(f32[2048,1024]{1,0:T(8,128)} %a_blk.1, f32[2048,512]{1,0:T(8,128)} %c_blk.1, f32[512,1024]{1,0:T(8,128)S(1)} %copy-done, f32[512,512]{1,0:T(8,128)S(1)} %copy-done.1, f32[2560,512]{1,0:T(8,128)} %get-tuple-element.12.ac_any, f32[2048,1024]{1,0:T(8,128)} %a_blk.1, ...), custom_call_target="tpu_custom_call" | custom-call | tf_op jit(solution)/shard_map/finish_a/pallas_call | solution.py:723
Async XLA Ops:
  0.6 291.3 %copy-start.2 = (f32[1024,512]{1,0:T(8,128)S(1)}, f32[1024,512]{1,0:T(8,128)}, u32[]{:S(2)}) copy-start(f32[1024,512]{1,0:T(8,128)} %b_ref.1) | copy-start | bytes 6291460
  292.0 3.6 %copy-start = (f32[512,1024]{1,0:T(8,128)S(1)}, f32[512,1024]{1,0:T(8,128)}, u32[]{:S(2)}) copy-start(f32[512,1024]{1,0:T(8,128)} %get-tuple-element.10.ar_any) | copy-start | bytes 6291460
  292.0 3.6 %copy-start.1 = (f32[512,512]{1,0:T(8,128)S(1)}, f32[512,512]{1,0:T(8,128)}, u32[]{:S(2)}) copy-start(f32[512,512]{1,0:T(8,128)} %get-tuple-element.11.cr_any) | copy-start | bytes 3145732

commit v2 on v1

--- a/solution.py
+++ b/solution.py
@@ -450,6 +450,7 @@
             drain(jnp.maximum(p - SLOTS, 0))
 
         early = blocks
+        beside = (chip == col_root(p) // cores) & jnp.logical_not(owner)
 
         @pl.when(jnp.logical_not(root))
         def _():
@@ -467,8 +468,11 @@
                 take(q, range(1))
 
             make_rows(p)
-            for i in range(tiles):
-                row_sends(p, i, start)
+
+            @pl.when(jnp.logical_not(beside))
+            def _():
+                for i in range(tiles):
+                    row_sends(p, i, start)
 
         @pl.when(owner)
         def _():
@@ -499,6 +503,11 @@
         @pl.when(p > 0)
         def _():
             update(q)
+
+        @pl.when(root & beside)
+        def _():
+            for i in range(tiles):
+                row_sends(p, i, start)
 
         if WITH_A:
             z_turn(p)
@@ -635,7 +644,7 @@
 
 
 def finish_kernel(
-    wide_a, tile, a_any, c_any, ar_any, cr_any, ac_any, a_blk, c_blk, ao_blk, co_blk,
+    wide_a, tile, a_any, c_any, ar_any, cr_any, ac_any, sums, a_blk, c_blk, b_blk, inv_blk, ao_blk, co_blk, bo_blk,
     col, rows, top, w, rows3, w3, sem,
 ):
     me_row = lax.axis_index("row")
@@ -671,12 +680,13 @@
         fetch(jnp.logical_not(top_row), ar_any, a_part, 2)
         fetch(top_row, c_any.at[first], c_part, 3)
         fetch(jnp.logical_not(top_row), cr_any, c_part, 3)
-        for i, dst in enumerate((top, col, a_part, c_part)):
-            fetched(dst, i)
-
+        fetched(top, 0)
         for s in range(count):
             inverse = pivot_inverse(top[part(s), part(s)], SPLIT)
             top[part(s), part(s)] = top[part(s), part(s)] - unit()
+            if s == 0:
+                for i, dst in ((1, col), (2, a_part), (3, c_part)):
+                    fetched(dst, i)
 
             @pl.when(top_row)
             def _():
@@ -703,6 +713,11 @@
         high, low = halves(w[...])
         w3[:, :wide_a], w3[:, wide_a : 2 * wide_a], w3[:, 2 * wide_a :] = high, high, low
 
+    b_squares = jnp.sum(jnp.sum(sums[0], axis=1, keepdims=True), axis=0, keepdims=True)
+    inv_squares = jnp.sum(jnp.sum(sums[1], axis=1, keepdims=True), axis=0, keepdims=True)
+    scale = jnp.sqrt(jnp.sqrt(inv_squares / b_squares))
+    bo_blk[...] = 0.5 * (scale * b_blk[...] + inv_blk[...] / scale)
+
     mine = pl.ds(pl.multiple_of(here * tile, tile), tile)
     taken = jnp.dot(w3[mine, :], rows3[...], preferred_element_type=jnp.float32)
     ao_blk[...] = a_blk[...] - taken[:, :a_cols]
@@ -715,21 +730,27 @@
         ao_blk[:, :wide_a] = (down == across).astype(jnp.float32) - taken[:, :wide_a]
 
 
-def finish_a(a_matrix, c_matrix, a_rows, c_rows, a_cols):
+def finish_all(a_matrix, c_matrix, b_matrix, a_rows, c_rows, a_cols, b_inverse, sums):
     height, width = a_matrix.shape
     c_width = c_matrix.shape[1]
     wide_a = a_cols.shape[1]
-    tile = PANEL
+    tile = min(2 * PANEL, height)
+    count = height // tile
+    b_height, b_width = b_matrix.shape
+    a_spec = pl.BlockSpec((tile, width), lambda i: (i, 0))
+    c_spec = pl.BlockSpec((tile, c_width), lambda i: (i, 0))
+    b_spec = pl.BlockSpec((b_height // count, b_width), lambda i: (i, 0))
     return pl.pallas_call(
         functools.partial(finish_kernel, wide_a, tile),
-        grid=(height // tile,),
+        grid=(count,),
         out_shape=[
             jax.ShapeDtypeStruct((height, width), jnp.float32),
             jax.ShapeDtypeStruct((height, c_width), jnp.float32),
+            jax.ShapeDtypeStruct((b_height, b_width), jnp.float32),
         ],
         in_specs=[pl.BlockSpec(memory_space=pl.ANY)] * 5
-        + [pl.BlockSpec((tile, width), lambda i: (i, 0)), pl.BlockSpec((tile, c_width), lambda i: (i, 0))],
-        out_specs=[pl.BlockSpec((tile, width), lambda i: (i, 0)), pl.BlockSpec((tile, c_width), lambda i: (i, 0))],
+        + [pl.BlockSpec(memory_space=pltpu.VMEM), a_spec, c_spec, b_spec, b_spec],
+        out_specs=[a_spec, c_spec, b_spec],
         scratch_shapes=[
             pltpu.VMEM((height, wide_a), jnp.float32),
             pltpu.VMEM((wide_a, width + c_width), jnp.float32),
@@ -739,18 +760,14 @@
             pltpu.VMEM((height, 3 * wide_a), jnp.bfloat16),
             pltpu.SemaphoreType.DMA((4,)),
         ],
-        compiler_params=pltpu.CompilerParams(vmem_limit_bytes=48 * 1024 * 1024),
-        name="finish_a",
-    )(a_matrix, c_matrix, a_rows, c_rows, a_cols, a_matrix, c_matrix)
+        compiler_params=pltpu.CompilerParams(vmem_limit_bytes=62 * 1024 * 1024),
+        name="finish_all",
+    )(a_matrix, c_matrix, a_rows, c_rows, a_cols, sums, a_matrix, c_matrix, b_matrix, b_inverse)
 
 
 def body(plan, a_matrix, b_matrix, c_matrix):
     b_inverse, sums, a_rows, c_rows, a_cols = sweep_b(plan, b_matrix, a_matrix, c_matrix)
-    a_swept, c_swept = finish_a(a_matrix, c_matrix, a_rows, c_rows, a_cols)
-    b_squares, inv_squares = jnp.sum(sums[0]), jnp.sum(sums[1])
-    scale = jnp.sqrt(jnp.sqrt(inv_squares / b_squares))
-    b_next = 0.5 * (scale * b_matrix + b_inverse / scale)
-    return (a_swept, c_swept, b_next)
+    return tuple(finish_all(a_matrix, c_matrix, b_matrix, a_rows, c_rows, a_cols, b_inverse, sums))
 
 
 def solution(mesh):

time: 324 us -> 317 us (0.978)
  other arithmetic: 4.88 us -> 0 us
    mul x1 -> x0, other arithmetic: 3.58 us -> none  [body(): b_next = 0.5 * (scale * b_matrix + b_inverse / scale)]
where the time goes in v2:
time: 317 us
  Pallas kernels  316 us (100%)
    pallas_call x1, Pallas kernels, sweep_b(): pl.pallas_call(functools.partial(sweep_kernel, plan, steps, wide_a, piece...  289 us
    pallas_call x1, Pallas kernels, finish_all(): pl.pallas_call(functools.partial(finish_kernel, wide_a, tile), grid=(coun...  27.8 us

profile of v2, /device:TPU:15, one launch (start us, length us, event | category | flops | bytes accessed | tf_op | source)
XLA Modules:
  0.0 317.2 jit_solution(10306244579743960067)
XLA Ops:
  0.6 288.6 %sweep_b.1 = (f32[1024,512]{1,0:T(8,128)}, f32[2,8,128]{2,1,0:T(8,128)}, f32[512,1024]{1,0:T(8,128)}, f32[512,512]{1,0:T(8,128)}, f32[2560,512]{1,0:T(8,128)}) custom-call(f32[1024,512]{1,0:T(8,128)} %b_blk.1, f32[2048,1024]{1,0:T(8,128)} %a_blk.1, f32[2048,512]{1,0:T(8,128)} %c_blk.1), custom_call_target="tpu_custom_call" | custom-call | tf_op jit(solution)/shard_map/sweep_b/pallas_call | solution.py:594
  289.2 27.8 %finish_all.1 = (f32[2048,1024]{1,0:T(8,128)}, f32[2048,512]{1,0:T(8,128)}, f32[1024,512]{1,0:T(8,128)}) custom-call(f32[2048,1024]{1,0:T(8,128)} %a_blk.1, f32[2048,512]{1,0:T(8,128)} %c_blk.1, f32[512,1024]{1,0:T(8,128)} %get-tuple-element.8.ar_any, f32[512,512]{1,0:T(8,128)} %get-tuple-element.9.cr_any, f32[2560,512]{1,0:T(8,128)} %get-tuple-element.10.ac_any, ...), custom_call_target="tpu_custom_call" | custom-call | tf_op jit(solution)/shard_map/finish_all/pallas_call | solution.py:743

commit v3 on v2

--- a/solution.py
+++ b/solution.py
@@ -271,23 +271,26 @@
                 def _():
                     r[p, j] = fresh - dot(step, r[q, j], SPLIT)
 
-    def make_w(p):
+    def make_w(p, i):
         j = p % tiles
+        mine = block(p + 1 + i)
 
         @pl.when(p == 0)
         def _():
-            t[...] = m[j]
+            t[...] = m[j, mine, :]
 
         @pl.when(p > 0)
         def _():
             q = jnp.maximum(p - 1, 0)
-            t[...] = m[j] - dot(w[q], r[q, j], SPLIT)
-
-        @pl.when(me_row == row_root(p))
-        def _():
-            t[block(p), :] = t[block(p), :] - unit()
-
-        w[p] = dot(t[...], x[...], SPLIT)
+            t[...] = m[j, mine, :] - dot(w[q, mine, :], r[q, j], SPLIT)
+
+        if i == blocks - 1:
+
+            @pl.when(me_row == row_root(p))
+            def _():
+                t[...] = t[...] - unit()
+
+        w[p, mine, :] = dot(t[...], x[...], SPLIT)
 
     def update(q):
         for j in range(tiles):
@@ -488,11 +491,9 @@
 
         @pl.when(owner)
         def _():
-            make_w(p)
             for i in range(blocks):
-                w_sends(p, i, start, ways=())
-            for i in range(blocks):
-                w_sends(p, i, start, across=False)
+                make_w(p, i)
+                w_sends(p, i, start)
 
         @pl.when(jnp.logical_not(root))
         def _():
@@ -611,7 +612,7 @@
             vmem((steps, height, PANEL), jnp.float32),
             vmem((steps, tiles, PANEL, PANEL), jnp.float32),
             vmem((PANEL, PANEL), jnp.float32),
-            vmem((height, PANEL), jnp.float32),
+            vmem((PANEL, PANEL), jnp.float32),
             vmem((plan.rows, 2, 8, 128), jnp.float32),
             vmem((plan.cols, 2, 8, 128), jnp.float32),
             dma((tiles,)),

time: 317 us -> 315 us (level)
  no operation moved by 1% of the time
where the time goes in v3:
time: 315 us; the launch traced here: 314 us
  Pallas kernels  314 us (100%)
    pallas_call x1, Pallas kernels, sweep_b(): pl.pallas_call(functools.partial(sweep_kernel, plan, steps, wide_a, piece...  286 us
    pallas_call x1, Pallas kernels, finish_all(): pl.pallas_call(functools.partial(finish_kernel, wide_a, tile), grid=(coun...  27.8 us

profile of v3, /device:TPU:15, one launch (start us, length us, event | category | flops | bytes accessed | tf_op | source)
XLA Modules:
  0.0 314.4 jit_solution(5806283575486431806)
XLA Ops:
  0.6 285.8 %sweep_b.1 = (f32[1024,512]{1,0:T(8,128)}, f32[2,8,128]{2,1,0:T(8,128)}, f32[512,1024]{1,0:T(8,128)}, f32[512,512]{1,0:T(8,128)}, f32[2560,512]{1,0:T(8,128)}) custom-call(f32[1024,512]{1,0:T(8,128)} %b_blk.1, f32[2048,1024]{1,0:T(8,128)} %a_blk.1, f32[2048,512]{1,0:T(8,128)} %c_blk.1), custom_call_target="tpu_custom_call" | custom-call | tf_op jit(solution)/shard_map/sweep_b/pallas_call | solution.py:595
  286.4 27.8 %finish_all.1 = (f32[2048,1024]{1,0:T(8,128)}, f32[2048,512]{1,0:T(8,128)}, f32[1024,512]{1,0:T(8,128)}) custom-call(f32[2048,1024]{1,0:T(8,128)} %a_blk.1, f32[2048,512]{1,0:T(8,128)} %c_blk.1, f32[512,1024]{1,0:T(8,128)} %get-tuple-element.8.ar_any, f32[512,512]{1,0:T(8,128)} %get-tuple-element.9.cr_any, f32[2560,512]{1,0:T(8,128)} %get-tuple-element.10.ac_any, ...), custom_call_target="tpu_custom_call" | custom-call | tf_op jit(solution)/shard_map/finish_all/pallas_call | solution.py:744
